TPU v7x, 32 devices: a whole 2x2x4 slice. The times are simulated.
32 devices in a mesh: sfc: 8 (over z, y), sub: 4 (over x, core).
Axes of the slice: x: 2, y: 2, z: 4, core: 2. Of those that a mesh axis runs over, the one named last changes fastest.
Arguments:
- vectors: float32 [64, 512, 256], P(None, ('sfc', 'sub')), may hold values from -10 to 10
- reaction: float32 [512, 256], P(('sfc', 'sub')), may hold values from 0.5 to 5
Outputs:
- basis: float32 [64, 512, 256], P(None, ('sfc', 'sub'))
- upper: float32 [64, 64], replicated
All inputs are finite; a program needn't handle non-finite values.
Results may differ from a plain program's by a relative error of at most 0.0003.
Values sent between devices are 32-bit elements; how exact they have to be, the bound alone decides.
A program may use at most 64 MiB of HBM per device.

v0:
```python
import math
import jax
import jax.numpy as jnp
from jax import lax
from jax.sharding import PartitionSpec as P

NY = 32
NL = 8
POWERS = 3
DELTA_MASS = 0.5


def with_halo(cells, sides, width):
    for axis, dim in sides:
        count = lax.axis_size(axis)
        ends = count - 1
        head = lax.slice_in_dim(cells, 0, width, axis=dim)
        tail = lax.slice_in_dim(cells, cells.shape[dim] - width, cells.shape[dim], axis=dim)
        cells = jnp.concatenate(
            [
                lax.ppermute(tail, axis, [(i, (i + 1) % count) for i in range(ends)]),
                cells,
                lax.ppermute(head, axis, [((i + 1) % count, i) for i in range(ends)]),
            ],
            axis=dim,
        )
    return cells


def line_tables(count):
    index = jnp.arange(count)
    offset = index[:, None] - index[None, :]
    near = (jnp.abs(offset) == 1).astype(jnp.float32)
    same = (offset == 0).astype(jnp.float32)
    mass = (4.0 * same + near) / 6.0
    stiff = 2.0 * same - near
    return (mass, stiff)


def tables(across, layers):
    mass_across, stiff_across = line_tables(across)
    mass_layers, stiff_layers = line_tables(layers)
    mass_plane = jnp.kron(mass_layers, mass_across)
    stiff_plane = (
        jnp.kron(mass_layers, stiff_across)
        + jnp.kron(stiff_layers, mass_across)
        + DELTA_MASS * mass_plane
    )
    return jnp.concatenate([mass_plane, stiff_plane], axis=1)


def plane_products(field, table):
    plane = table.shape[0]
    both = jnp.einsum("kzp,pq->kzq", field, table, precision=lax.Precision.HIGHEST)
    return (both[..., :plane], both[..., plane:])


def operate(field, reaction, table):
    massed, mixed = plane_products(field, table)
    edge_term = mixed / 6.0 - massed
    padded = with_halo(edge_term, ((("sfc", "sub"), 1),), 1)
    neighbours = padded[:, :-2] + padded[:, 2:]
    return neighbours + 4.0 / 6.0 * mixed + 2.0 * massed + reaction[None] * field


def whole_factor(local):
    gram = jnp.dot(local, local.T, precision=lax.Precision.HIGHEST)
    total = lax.psum(gram, ("sfc", "sub"))
    return jnp.linalg.cholesky(total)


def lower_solve(lower, block):
    return lax.linalg.triangular_solve(lower, block, left_side=True, lower=True)


def per_device(vectors, reaction):
    table = tables(NY, NL)
    field = vectors
    for _ in range(POWERS):
        field = operate(field, reaction, table)
    local = field.reshape(field.shape[0], -1)
    lower_one = whole_factor(local)
    first = lower_solve(lower_one, local)
    lower_two = whole_factor(first)
    second = lower_solve(lower_two, first)
    scale = math.sqrt(lax.axis_size("sfc") * lax.axis_size("sub") * local.shape[1])
    upper = jnp.dot(lower_one, lower_two, precision=lax.Precision.HIGHEST).T / scale
    return ((second * scale).reshape(vectors.shape), upper)


def solution(mesh):
    placed = (P(None, ("sfc", "sub"), None), P(("sfc", "sub"), None))
    return jax.shard_map(
        per_device,
        mesh=mesh,
        in_specs=placed,
        out_specs=(P(None, ("sfc", "sub"), None), P()),
        check_vma=False,
    )
```

profile of v0, /device:TPU:0, one launch (start us, length us, event | category | flops | bytes accessed | tf_op | source)
XLA Modules:
  0.0 152.5 jit_solution(1561632378919360733)
XLA Ops:
  0.7 0.3 broadcast_multiply_fusion
  1.0 0.0 copy-start
  1.0 0.3 mul.143
  1.3 0.3 add.78
  1.6 0.5 copy-done
  2.2 2.3 %convolution_bitcast_fusion = f32[64,16,512]{2,0,1:T(8,128)S(1)} fusion(f32[64,16,256]{2,1,0:T(8,128)S(1)} %copy-done, f32[256,256]{1,0:T(8,128)S(1)} %multiply_add_fusion.1, f32[256,256]{1,0:T(8,128)S(1)} %mul.143), kind=kOutput, calls=%fused_computation.1 | convolution fusion | flops 1610743808 | bytes 3670016 | tf_op jit(solution)/shard_map/kzp,pq->kzq/dot_general | solution.py:54
  4.5 0.0 copy-start.1
  4.5 0.2 multiply_subtract_fusion.2
  4.7 2.4 %collective-permute-start = (f32[64,1,256]{2,0,1:T(8,128)S(1)}, f32[64,1,256]{2,0,1:T(8,128)S(1)}, u32[]{:S(2)}, u32[]{:S(2)}) collective-permute-start(f32[64,1,256]{2,0,1:T(8,128)S(1)} %get-tuple-element.8), channel_id=1, source_target_pairs={{0,1},{1,2},{2,3},{3,4},{4,5},{5,6},{6,7},{7,8},{8,9},{9,10},{10,1... | collective-permute-start | bytes 196616 | tf_op jit(solution)/shard_map/ppermute | solution.py:21
  7.1 1.3 collective-permute-start.1
  8.4 0.0 collective-permute-done
  8.4 3.9 %collective-permute-done.1 = f32[64,1,256]{2,0,1:T(8,128)S(1)} collective-permute-done((f32[64,1,256]{2,0,1:T(8,128)S(1)}, f32[64,1,256]{2,0,1:T(8,128)S(1)}, u32[]{:S(2)}, u32[]{:S(2)}) %collective-permute-start.1) | collective-permute-done | bytes 65568 | tf_op jit(solution)/shard_map/ppermute | solution.py:23
  12.3 0.0 copy-done.1
  12.3 0.8 fusion.11
  13.2 1.8 %fusion.14 = f32[64,16,512]{2,0,1:T(8,128)S(1)} fusion(f32[64,16,256]{2,0,1:T(8,128)S(1)} %fusion.11, f32[256,256]{1,0:T(8,128)S(1)} %multiply_add_fusion.1, f32[256,256]{1,0:T(8,128)S(1)} %mul.143), kind=kOutput, calls=%fused_computation.30 | convolution fusion | flops 1610743808 | bytes 3670016 | tf_op jit(solution)/shard_map/kzp,pq->kzq/dot_general | solution.py:54
  15.0 0.2 multiply_subtract_fusion.1
  15.2 4.8 %collective-permute-start.2 = (f32[64,1,256]{2,0,1:T(8,128)S(1)}, f32[64,1,256]{2,0,1:T(8,128)S(1)}, u32[]{:S(2)}, u32[]{:S(2)}) collective-permute-start(f32[64,1,256]{2,0,1:T(8,128)S(1)} %get-tuple-element.6), channel_id=1, source_target_pairs={{0,1},{1,2},{2,3},{3,4},{4,5},{5,6},{6,7},{7,8},{8,9},{9,10},{10,1... | collective-permute-start | bytes 196616 | tf_op jit(solution)/shard_map/ppermute | solution.py:21
  20.0 1.3 collective-permute-start.3
  21.3 0.0 collective-permute-done.2
  21.4 1.8 %collective-permute-done.3 = f32[64,1,256]{2,0,1:T(8,128)S(1)} collective-permute-done((f32[64,1,256]{2,0,1:T(8,128)S(1)}, f32[64,1,256]{2,0,1:T(8,128)S(1)}, u32[]{:S(2)}, u32[]{:S(2)}) %collective-permute-start.3) | collective-permute-done | bytes 65568 | tf_op jit(solution)/shard_map/ppermute | solution.py:23
  23.2 0.3 fusion.7
  23.5 1.8 %fusion.13 = f32[64,16,512]{2,0,1:T(8,128)S(1)} fusion(f32[64,16,256]{2,0,1:T(8,128)S(1)} %fusion.7, f32[256,256]{1,0:T(8,128)S(1)} %multiply_add_fusion.1, f32[256,256]{1,0:T(8,128)S(1)} %mul.143), kind=kOutput, calls=%fused_computation.29 | convolution fusion | flops 1610743808 | bytes 3670016 | tf_op jit(solution)/shard_map/kzp,pq->kzq/dot_general | solution.py:54
  25.4 0.2 multiply_subtract_fusion
  25.6 5.1 %collective-permute-start.4 = (f32[64,1,256]{2,0,1:T(8,128)S(1)}, f32[64,1,256]{2,0,1:T(8,128)S(1)}, u32[]{:S(2)}, u32[]{:S(2)}) collective-permute-start(f32[64,1,256]{2,0,1:T(8,128)S(1)} %get-tuple-element.4), channel_id=1, source_target_pairs={{0,1},{1,2},{2,3},{3,4},{4,5},{5,6},{6,7},{7,8},{8,9},{9,10},{10,1... | collective-permute-start | bytes 196616 | tf_op jit(solution)/shard_map/ppermute | solution.py:21
  30.7 1.3 collective-permute-start.5
  32.0 0.0 collective-permute-done.4
  32.0 1.8 %collective-permute-done.5 = f32[64,1,256]{2,0,1:T(8,128)S(1)} collective-permute-done((f32[64,1,256]{2,0,1:T(8,128)S(1)}, f32[64,1,256]{2,0,1:T(8,128)S(1)}, u32[]{:S(2)}, u32[]{:S(2)}) %collective-permute-start.5) | collective-permute-done | bytes 65568 | tf_op jit(solution)/shard_map/ppermute | solution.py:23
  33.8 0.3 fusion.3
  34.1 1.0 convolution_bitcast_fusion.1
  35.1 45.9 %psum.14 = f32[64,64]{0,1:T(8,128)S(1)} all-reduce(f32[64,64]{0,1:T(8,128)S(1)} %convolution_bitcast_fusion.1), channel_id=1, replica_groups=mesh['sfc'=8,'sub'=4] {'sfc','sub'}, use_global_device_ids=true, to_apply=%region_0.1 | all-reduce | flops 4096 | bytes 32768 | tf_op jit(solution)/shard_map/psum | solution.py:68
  81.0 0.1 copy.25
  81.1 5.8 %cholesky.44 = f32[64,64]{1,0:T(8,128)S(1)} custom-call(f32[64,64]{1,0:T(8,128)S(1)} %fusion.19), custom_call_target="Cholesky" | custom-call | tf_op jit(solution)/shard_map/jit(cholesky)/cholesky | solution.py:69
  87.0 0.6 compare_reduce_fusion.1
  87.6 0.7 fusion.23
  88.3 4.9 %custom-call.6 = f32[1,64,64]{1,2,0:T(8,128)S(1)} custom-call(f32[1,64,64]{2,1,0:T(8,128)S(1)} %fusion.23), custom_call_target="InvertDiagBlocksLowerTriangular" | custom-call | tf_op jit(solution)/shard_map/triangular_solve/custom-call.0 | solution.py:73
  93.2 0.1 copy.36
  93.3 1.0 fusion.17
  94.3 1.0 fusion.44
  95.3 40.3 %psum.15 = f32[64,64]{0,1:T(8,128)S(1)} all-reduce(f32[64,64]{0,1:T(8,128)S(1)} %fusion.44), channel_id=1, replica_groups=mesh['sfc'=8,'sub'=4] {'sfc','sub'}, use_global_device_ids=true, to_apply=%region_3.6 | all-reduce | flops 4096 | bytes 32768 | tf_op jit(solution)/shard_map/psum | solution.py:68
  135.6 0.1 copy.28
  135.7 5.8 %cholesky.55 = f32[64,64]{1,0:T(8,128)S(1)} custom-call(f32[64,64]{1,0:T(8,128)S(1)} %fusion.16), custom_call_target="Cholesky" | custom-call | tf_op jit(solution)/shard_map/jit(cholesky)/cholesky | solution.py:69
  141.6 0.7 compare_reduce_fusion
  142.3 2.2 %convolution_multiply_fusion.1 = f32[64,64]{1,0:T(8,128)} fusion(f32[64,64]{1,0:T(8,128)S(1)} %cholesky.55, f32[64,64]{1,0:T(8,128)S(1)} %cholesky.44, pred[]{:T(512)} %compare_reduce_fusion, pred[]{:T(512)} %compare_reduce_fusion.1), kind=kOutput, calls=%fused_computation.2 | convolution fusion | flops 3174400 | bytes 49154 | tf_op jit(solution)/shard_map/dot_general | solution.py:87
  144.5 0.7 select_bitcast_fusion
  145.2 4.9 %custom-call.7 = f32[1,64,64]{1,2,0:T(8,128)S(1)} custom-call(f32[1,64,64]{2,1,0:T(8,128)S(1)} %select_bitcast_fusion), custom_call_target="InvertDiagBlocksLowerTriangular" | custom-call | tf_op jit(solution)/shard_map/triangular_solve/custom-call.0 | solution.py:73
  150.1 1.1 convolution_multiply_fusion
  151.2 1.3 copy.37
  (10 shorter events, 0.2 us)
Async XLA Ops:
  1.0 1.2 copy-start
  4.5 7.8 %copy-start.1 = (f32[16,256]{1,0:T(8,128)S(1)}, f32[16,256]{1,0:T(8,128)}, u32[]{:S(2)}) copy-start(f32[16,256]{1,0:T(8,128)} %param.6) | copy-start | bytes 49156
  4.7 3.7 %collective-permute-start = (f32[64,1,256]{2,0,1:T(8,128)S(1)}, f32[64,1,256]{2,0,1:T(8,128)S(1)}, u32[]{:S(2)}, u32[]{:S(2)}) collective-permute-start(f32[64,1,256]{2,0,1:T(8,128)S(1)} %get-tuple-element.8), channel_id=1, source_target_pairs={{0,1},{1,2},{2,3},{3,4},{4,5},{5,6},{6,7},{7,8},{8,9},{9,10},{10,1... | collective-permute-start | bytes 196616 | tf_op jit(solution)/shard_map/ppermute | solution.py:21
  7.1 5.2 %collective-permute-start.1 = (f32[64,1,256]{2,0,1:T(8,128)S(1)}, f32[64,1,256]{2,0,1:T(8,128)S(1)}, u32[]{:S(2)}, u32[]{:S(2)}) collective-permute-start(f32[64,1,256]{2,0,1:T(8,128)S(1)} %get-tuple-element.9), channel_id=1, source_target_pairs={{1,0},{2,1},{3,2},{4,3},{5,4},{6,5},{7,6},{8,7},{9,8},{10,9},{11,1... | collective-permute-start | bytes 196616 | tf_op jit(solution)/shard_map/ppermute | solution.py:23
  15.2 6.2 %collective-permute-start.2 = (f32[64,1,256]{2,0,1:T(8,128)S(1)}, f32[64,1,256]{2,0,1:T(8,128)S(1)}, u32[]{:S(2)}, u32[]{:S(2)}) collective-permute-start(f32[64,1,256]{2,0,1:T(8,128)S(1)} %get-tuple-element.6), channel_id=1, source_target_pairs={{0,1},{1,2},{2,3},{3,4},{4,5},{5,6},{6,7},{7,8},{8,9},{9,10},{10,1... | collective-permute-start | bytes 196616 | tf_op jit(solution)/shard_map/ppermute | solution.py:21
  20.0 3.1 %collective-permute-start.3 = (f32[64,1,256]{2,0,1:T(8,128)S(1)}, f32[64,1,256]{2,0,1:T(8,128)S(1)}, u32[]{:S(2)}, u32[]{:S(2)}) collective-permute-start(f32[64,1,256]{2,0,1:T(8,128)S(1)} %get-tuple-element.7), channel_id=1, source_target_pairs={{1,0},{2,1},{3,2},{4,3},{5,4},{6,5},{7,6},{8,7},{9,8},{10,9},{11,1... | collective-permute-start | bytes 196616 | tf_op jit(solution)/shard_map/ppermute | solution.py:23
  25.6 6.4 %collective-permute-start.4 = (f32[64,1,256]{2,0,1:T(8,128)S(1)}, f32[64,1,256]{2,0,1:T(8,128)S(1)}, u32[]{:S(2)}, u32[]{:S(2)}) collective-permute-start(f32[64,1,256]{2,0,1:T(8,128)S(1)} %get-tuple-element.4), channel_id=1, source_target_pairs={{0,1},{1,2},{2,3},{3,4},{4,5},{5,6},{6,7},{7,8},{8,9},{9,10},{10,1... | collective-permute-start | bytes 196616 | tf_op jit(solution)/shard_map/ppermute | solution.py:21
  30.7 3.1 %collective-permute-start.5 = (f32[64,1,256]{2,0,1:T(8,128)S(1)}, f32[64,1,256]{2,0,1:T(8,128)S(1)}, u32[]{:S(2)}, u32[]{:S(2)}) collective-permute-start(f32[64,1,256]{2,0,1:T(8,128)S(1)} %get-tuple-element.5), channel_id=1, source_target_pairs={{1,0},{2,1},{3,2},{4,3},{5,4},{6,5},{7,6},{8,7},{9,8},{10,9},{11,1... | collective-permute-start | bytes 196616 | tf_op jit(solution)/shard_map/ppermute | solution.py:23
where the time goes:
time: 153 us; the launch traced here: 152 us
  blocking collectives  86.2 us (56%)
  other arithmetic  26.6 us (17%)
  starting transfers between devices  16.2 us (11%)
  matrix products  12.2 us (8%)
  waiting for transfers between devices  7.62 us (5%)
  local copies, waits for them, and re-layouts  2.74 us (2%)
    psum x2, blocking collectives, whole_factor(): total = lax.psum(gram, ('sfc', 'sub'))  86.2 us
    another operation x6, other arithmetic, whole_factor(): return jnp.linalg.cholesky(total)  13.1 us
    ppermute x3, starting transfers between devices, with_halo(): lax.ppermute(tail, axis, [(i, (i + 1) % count) for i in range(ends)])  12.4 us
    another operation x4, other arithmetic, lower_solve(): return lax.linalg.triangular_solve(lower, block, left_side=True, lower=True)  11.1 us
    ppermute x3, waiting for transfers between devices, with_halo(): lax.ppermute(head, axis, [((i + 1) % count, i) for i in range(ends)])  7.61 us
    dot_general x3, matrix products, plane_products(): jnp.einsum('kzp,pq->kzq', field, table, precision=lax.Precision.HIGHEST)  5.98 us
    ppermute x3, starting transfers between devices, with_halo(): lax.ppermute(head, axis, [((i + 1) % count, i) for i in range(ends)])  3.88 us
  transfers between devices with their start and end apart: 6, of which 3 were waited for; matrix products, arithmetic and copies ran while one was open for 0% of the time, Pallas kernels for 0%

commit v1 on v0

--- a/solution.py
+++ b/solution.py
@@ -65,7 +65,7 @@
 
 def whole_factor(local):
     gram = jnp.dot(local, local.T, precision=lax.Precision.HIGHEST)
-    total = lax.psum(gram, ("sfc", "sub"))
+    total = lax.psum(lax.psum(gram, "sub"), "sfc")
     return jnp.linalg.cholesky(total)
 
 

time: 153 us -> 163 us (1.065)
  blocking collectives: 86.2 us -> 96.3 us
    psum x2 -> x4, blocking collectives: 86.2 us -> 96.3 us  [whole_factor(): total = lax.psum(lax.psum(gram, 'sub'), 'sfc')]
where the time goes in v1:
time: 163 us
  blocking collectives  96.3 us (59%)
  other arithmetic  26.6 us (16%)
  starting transfers between devices  16.2 us (10%)
  matrix products  12.2 us (7%)
  waiting for transfers between devices  7.62 us (5%)
  local copies, waits for them, and re-layouts  2.75 us (2%)
    psum x4, blocking collectives, whole_factor(): total = lax.psum(lax.psum(gram, 'sub'), 'sfc')  96.3 us
    another operation x6, other arithmetic, whole_factor(): return jnp.linalg.cholesky(total)  13.1 us
    ppermute x3, starting transfers between devices, with_halo(): lax.ppermute(tail, axis, [(i, (i + 1) % count) for i in range(ends)])  12.4 us
    another operation x4, other arithmetic, lower_solve(): return lax.linalg.triangular_solve(lower, block, left_side=True, lower=True)  11.1 us
    ppermute x3, waiting for transfers between devices, with_halo(): lax.ppermute(head, axis, [((i + 1) % count, i) for i in range(ends)])  7.61 us
    dot_general x3, matrix products, plane_products(): jnp.einsum('kzp,pq->kzq', field, table, precision=lax.Precision.HIGHEST)  5.98 us
    ppermute x3, starting transfers between devices, with_halo(): lax.ppermute(head, axis, [((i + 1) % count, i) for i in range(ends)])  3.88 us
  transfers between devices with their start and end apart: 6, of which 3 were waited for; matrix products, arithmetic and copies ran while one was open for 0% of the time, Pallas kernels for 0%

profile of v1, /device:TPU:0, one launch (start us, length us, event | category | flops | bytes accessed | tf_op | source)
XLA Modules:
  0.0 162.6 jit_solution(15277902875392091801)
XLA Ops:
  0.7 0.3 broadcast_multiply_fusion
  1.0 0.0 copy-start
  1.0 0.3 mul.143
  1.3 0.3 add.82
  1.6 0.5 copy-done
  2.2 2.3 %convolution_bitcast_fusion = f32[64,16,512]{2,0,1:T(8,128)S(1)} fusion(f32[64,16,256]{2,1,0:T(8,128)S(1)} %copy-done, f32[256,256]{1,0:T(8,128)S(1)} %multiply_add_fusion.1, f32[256,256]{1,0:T(8,128)S(1)} %mul.143), kind=kOutput, calls=%fused_computation.1 | convolution fusion | flops 1610743808 | bytes 3670016 | tf_op jit(solution)/shard_map/kzp,pq->kzq/dot_general | solution.py:54
  4.5 0.0 copy-start.1
  4.5 0.2 multiply_subtract_fusion.2
  4.7 2.4 %collective-permute-start = (f32[64,1,256]{2,0,1:T(8,128)S(1)}, f32[64,1,256]{2,0,1:T(8,128)S(1)}, u32[]{:S(2)}, u32[]{:S(2)}) collective-permute-start(f32[64,1,256]{2,0,1:T(8,128)S(1)} %get-tuple-element.8), channel_id=1, source_target_pairs={{0,1},{1,2},{2,3},{3,4},{4,5},{5,6},{6,7},{7,8},{8,9},{9,10},{10,1... | collective-permute-start | bytes 196616 | tf_op jit(solution)/shard_map/ppermute | solution.py:21
  7.1 1.3 collective-permute-start.1
  8.4 0.0 collective-permute-done
  8.4 3.9 %collective-permute-done.1 = f32[64,1,256]{2,0,1:T(8,128)S(1)} collective-permute-done((f32[64,1,256]{2,0,1:T(8,128)S(1)}, f32[64,1,256]{2,0,1:T(8,128)S(1)}, u32[]{:S(2)}, u32[]{:S(2)}) %collective-permute-start.1) | collective-permute-done | bytes 65568 | tf_op jit(solution)/shard_map/ppermute | solution.py:23
  12.3 0.0 copy-done.1
  12.3 0.8 fusion.11
  13.2 1.8 %fusion.14 = f32[64,16,512]{2,0,1:T(8,128)S(1)} fusion(f32[64,16,256]{2,0,1:T(8,128)S(1)} %fusion.11, f32[256,256]{1,0:T(8,128)S(1)} %multiply_add_fusion.1, f32[256,256]{1,0:T(8,128)S(1)} %mul.143), kind=kOutput, calls=%fused_computation.30 | convolution fusion | flops 1610743808 | bytes 3670016 | tf_op jit(solution)/shard_map/kzp,pq->kzq/dot_general | solution.py:54
  15.0 0.2 multiply_subtract_fusion.1
  15.2 4.8 %collective-permute-start.2 = (f32[64,1,256]{2,0,1:T(8,128)S(1)}, f32[64,1,256]{2,0,1:T(8,128)S(1)}, u32[]{:S(2)}, u32[]{:S(2)}) collective-permute-start(f32[64,1,256]{2,0,1:T(8,128)S(1)} %get-tuple-element.6), channel_id=1, source_target_pairs={{0,1},{1,2},{2,3},{3,4},{4,5},{5,6},{6,7},{7,8},{8,9},{9,10},{10,1... | collective-permute-start | bytes 196616 | tf_op jit(solution)/shard_map/ppermute | solution.py:21
  20.0 1.3 collective-permute-start.3
  21.3 0.0 collective-permute-done.2
  21.4 1.8 %collective-permute-done.3 = f32[64,1,256]{2,0,1:T(8,128)S(1)} collective-permute-done((f32[64,1,256]{2,0,1:T(8,128)S(1)}, f32[64,1,256]{2,0,1:T(8,128)S(1)}, u32[]{:S(2)}, u32[]{:S(2)}) %collective-permute-start.3) | collective-permute-done | bytes 65568 | tf_op jit(solution)/shard_map/ppermute | solution.py:23
  23.2 0.3 fusion.7
  23.5 1.8 %fusion.13 = f32[64,16,512]{2,0,1:T(8,128)S(1)} fusion(f32[64,16,256]{2,0,1:T(8,128)S(1)} %fusion.7, f32[256,256]{1,0:T(8,128)S(1)} %multiply_add_fusion.1, f32[256,256]{1,0:T(8,128)S(1)} %mul.143), kind=kOutput, calls=%fused_computation.29 | convolution fusion | flops 1610743808 | bytes 3670016 | tf_op jit(solution)/shard_map/kzp,pq->kzq/dot_general | solution.py:54
  25.4 0.2 multiply_subtract_fusion
  25.6 5.1 %collective-permute-start.4 = (f32[64,1,256]{2,0,1:T(8,128)S(1)}, f32[64,1,256]{2,0,1:T(8,128)S(1)}, u32[]{:S(2)}, u32[]{:S(2)}) collective-permute-start(f32[64,1,256]{2,0,1:T(8,128)S(1)} %get-tuple-element.4), channel_id=1, source_target_pairs={{0,1},{1,2},{2,3},{3,4},{4,5},{5,6},{6,7},{7,8},{8,9},{9,10},{10,1... | collective-permute-start | bytes 196616 | tf_op jit(solution)/shard_map/ppermute | solution.py:21
  30.7 1.3 collective-permute-start.5
  32.0 0.0 collective-permute-done.4
  32.0 1.8 %collective-permute-done.5 = f32[64,1,256]{2,0,1:T(8,128)S(1)} collective-permute-done((f32[64,1,256]{2,0,1:T(8,128)S(1)}, f32[64,1,256]{2,0,1:T(8,128)S(1)}, u32[]{:S(2)}, u32[]{:S(2)}) %collective-permute-start.5) | collective-permute-done | bytes 65568 | tf_op jit(solution)/shard_map/ppermute | solution.py:23
  33.8 0.3 fusion.3
  34.1 1.0 convolution_bitcast_fusion.1
  35.1 15.6 %psum.28 = f32[64,64]{0,1:T(8,128)S(1)} all-reduce(f32[64,64]{0,1:T(8,128)S(1)} %convolution_bitcast_fusion.1), channel_id=1, replica_groups=mesh['sfc'=8,'sub'=4] {'sub'}, use_global_device_ids=true, to_apply=%region_0.1 | all-reduce | flops 4096 | bytes 32768 | tf_op jit(solution)/shard_map/psum | solution.py:68
  50.8 37.4 %psum.29 = f32[64,64]{0,1:T(8,128)S(1)} all-reduce(f32[64,64]{0,1:T(8,128)S(1)} %psum.28), channel_id=1, replica_groups=mesh['sfc'=8,'sub'=4] {'sfc'}, use_global_device_ids=true, to_apply=%region_1.2 | all-reduce | flops 4096 | bytes 32768 | tf_op jit(solution)/shard_map/psum | solution.py:68
  88.1 0.1 copy.25
  88.2 5.8 %cholesky.44 = f32[64,64]{1,0:T(8,128)S(1)} custom-call(f32[64,64]{1,0:T(8,128)S(1)} %fusion.19), custom_call_target="Cholesky" | custom-call | tf_op jit(solution)/shard_map/jit(cholesky)/cholesky | solution.py:69
  94.1 0.6 compare_reduce_fusion.1
  94.7 0.7 fusion.23
  95.4 4.9 %custom-call.6 = f32[1,64,64]{1,2,0:T(8,128)S(1)} custom-call(f32[1,64,64]{2,1,0:T(8,128)S(1)} %fusion.23), custom_call_target="InvertDiagBlocksLowerTriangular" | custom-call | tf_op jit(solution)/shard_map/triangular_solve/custom-call.0 | solution.py:73
  100.3 0.1 copy.36
  100.4 1.0 fusion.17
  101.5 1.0 fusion.44
  102.4 10.3 %psum.30 = f32[64,64]{0,1:T(8,128)S(1)} all-reduce(f32[64,64]{0,1:T(8,128)S(1)} %fusion.44), channel_id=1, replica_groups=mesh['sfc'=8,'sub'=4] {'sub'}, use_global_device_ids=true, to_apply=%region_4.7 | all-reduce | flops 4096 | bytes 32768 | tf_op jit(solution)/shard_map/psum | solution.py:68
  112.7 33.0 %psum.31 = f32[64,64]{0,1:T(8,128)S(1)} all-reduce(f32[64,64]{0,1:T(8,128)S(1)} %psum.30), channel_id=1, replica_groups=mesh['sfc'=8,'sub'=4] {'sfc'}, use_global_device_ids=true, to_apply=%region_5.8 | all-reduce | flops 4096 | bytes 32768 | tf_op jit(solution)/shard_map/psum | solution.py:68
  145.7 0.1 copy.28
  145.8 5.8 %cholesky.55 = f32[64,64]{1,0:T(8,128)S(1)} custom-call(f32[64,64]{1,0:T(8,128)S(1)} %fusion.16), custom_call_target="Cholesky" | custom-call | tf_op jit(solution)/shard_map/jit(cholesky)/cholesky | solution.py:69
  151.7 0.7 compare_reduce_fusion
  152.4 2.2 %convolution_multiply_fusion.1 = f32[64,64]{1,0:T(8,128)} fusion(f32[64,64]{1,0:T(8,128)S(1)} %cholesky.55, f32[64,64]{1,0:T(8,128)S(1)} %cholesky.44, pred[]{:T(512)} %compare_reduce_fusion, pred[]{:T(512)} %compare_reduce_fusion.1), kind=kOutput, calls=%fused_computation.2 | convolution fusion | flops 3174400 | bytes 49154 | tf_op jit(solution)/shard_map/dot_general | solution.py:87
  154.6 0.7 select_bitcast_fusion
  155.3 4.9 %custom-call.7 = f32[1,64,64]{1,2,0:T(8,128)S(1)} custom-call(f32[1,64,64]{2,1,0:T(8,128)S(1)} %select_bitcast_fusion), custom_call_target="InvertDiagBlocksLowerTriangular" | custom-call | tf_op jit(solution)/shard_map/triangular_solve/custom-call.0 | solution.py:73
  160.2 1.0 convolution_multiply_fusion
  161.3 1.3 copy.37
  (10 shorter events, 0.2 us)
Async XLA Ops:
  1.0 1.2 copy-start
  4.5 7.8 %copy-start.1 = (f32[16,256]{1,0:T(8,128)S(1)}, f32[16,256]{1,0:T(8,128)}, u32[]{:S(2)}) copy-start(f32[16,256]{1,0:T(8,128)} %param.6) | copy-start | bytes 49156
  4.7 3.7 %collective-permute-start = (f32[64,1,256]{2,0,1:T(8,128)S(1)}, f32[64,1,256]{2,0,1:T(8,128)S(1)}, u32[]{:S(2)}, u32[]{:S(2)}) collective-permute-start(f32[64,1,256]{2,0,1:T(8,128)S(1)} %get-tuple-element.8), channel_id=1, source_target_pairs={{0,1},{1,2},{2,3},{3,4},{4,5},{5,6},{6,7},{7,8},{8,9},{9,10},{10,1... | collective-permute-start | bytes 196616 | tf_op jit(solution)/shard_map/ppermute | solution.py:21
  7.1 5.2 %collective-permute-start.1 = (f32[64,1,256]{2,0,1:T(8,128)S(1)}, f32[64,1,256]{2,0,1:T(8,128)S(1)}, u32[]{:S(2)}, u32[]{:S(2)}) collective-permute-start(f32[64,1,256]{2,0,1:T(8,128)S(1)} %get-tuple-element.9), channel_id=1, source_target_pairs={{1,0},{2,1},{3,2},{4,3},{5,4},{6,5},{7,6},{8,7},{9,8},{10,9},{11,1... | collective-permute-start | bytes 196616 | tf_op jit(solution)/shard_map/ppermute | solution.py:23
  15.2 6.2 %collective-permute-start.2 = (f32[64,1,256]{2,0,1:T(8,128)S(1)}, f32[64,1,256]{2,0,1:T(8,128)S(1)}, u32[]{:S(2)}, u32[]{:S(2)}) collective-permute-start(f32[64,1,256]{2,0,1:T(8,128)S(1)} %get-tuple-element.6), channel_id=1, source_target_pairs={{0,1},{1,2},{2,3},{3,4},{4,5},{5,6},{6,7},{7,8},{8,9},{9,10},{10,1... | collective-permute-start | bytes 196616 | tf_op jit(solution)/shard_map/ppermute | solution.py:21
  20.0 3.1 %collective-permute-start.3 = (f32[64,1,256]{2,0,1:T(8,128)S(1)}, f32[64,1,256]{2,0,1:T(8,128)S(1)}, u32[]{:S(2)}, u32[]{:S(2)}) collective-permute-start(f32[64,1,256]{2,0,1:T(8,128)S(1)} %get-tuple-element.7), channel_id=1, source_target_pairs={{1,0},{2,1},{3,2},{4,3},{5,4},{6,5},{7,6},{8,7},{9,8},{10,9},{11,1... | collective-permute-start | bytes 196616 | tf_op jit(solution)/shard_map/ppermute | solution.py:23
  25.6 6.4 %collective-permute-start.4 = (f32[64,1,256]{2,0,1:T(8,128)S(1)}, f32[64,1,256]{2,0,1:T(8,128)S(1)}, u32[]{:S(2)}, u32[]{:S(2)}) collective-permute-start(f32[64,1,256]{2,0,1:T(8,128)S(1)} %get-tuple-element.4), channel_id=1, source_target_pairs={{0,1},{1,2},{2,3},{3,4},{4,5},{5,6},{6,7},{7,8},{8,9},{9,10},{10,1... | collective-permute-start | bytes 196616 | tf_op jit(solution)/shard_map/ppermute | solution.py:21
  30.7 3.1 %collective-permute-start.5 = (f32[64,1,256]{2,0,1:T(8,128)S(1)}, f32[64,1,256]{2,0,1:T(8,128)S(1)}, u32[]{:S(2)}, u32[]{:S(2)}) collective-permute-start(f32[64,1,256]{2,0,1:T(8,128)S(1)} %get-tuple-element.5), channel_id=1, source_target_pairs={{1,0},{2,1},{3,2},{4,3},{5,4},{6,5},{7,6},{8,7},{9,8},{10,9},{11,1... | collective-permute-start | bytes 196616 | tf_op jit(solution)/shard_map/ppermute | solution.py:23
